TPU v7x, 32 devices: a whole 2x2x4 slice. The times are simulated.
32 devices in a mesh: seq: 4 (over y, x), exp: 8 (over z, core).
Axes of the slice: x: 2, y: 2, z: 4, core: 2. Of those that a mesh axis runs over, the one named last changes fastest.
Arguments:
- tokens: bfloat16 [2, 24576, 1024], P(None, ('seq', 'exp')), may hold values from -60 to 60
- router: bfloat16 [1024, 64], replicated, may hold values from -0.25 to 0.25
- w_in: bfloat16 [16, 1024, 4096], P('exp', None, 'seq'), may hold values from -0.1875 to 0.1875
- w_out: bfloat16 [16, 4096, 1024], P('exp', 'seq'), may hold values from -0.09375 to 0.09375
- grad_out: bfloat16 [2, 24576, 1024], P(None, ('seq', 'exp')), may hold values from -6 to 6
Outputs:
- mixed: bfloat16 [2, 24576, 1024], P(None, ('seq', 'exp'))
- grad_tokens: bfloat16 [2, 24576, 1024], P(None, ('seq', 'exp'))
- grad_router: float32 [1024, 64], P(('seq', 'exp'))
- grad_w_in: bfloat16 [16, 1024, 4096], P('exp', None, 'seq')
- grad_w_out: bfloat16 [16, 4096, 1024], P('exp', 'seq')
All inputs are finite; a program needn't handle non-finite values.
Results may differ from a plain program's by a relative error of at most 0.018.
Values may be sent and summed in bfloat16 or wider, within the bound.
A program may use at most 128 MiB of HBM per device.

v0:
```python
import jax
import jax.numpy as jnp
from jax import lax
from jax.sharding import PartitionSpec as P


def on_device(tokens, router, w_in, w_out, grad_out):
    clips, tok_rows, width = tokens.shape
    slot_total = router.shape[1]
    owned = slot_total // lax.axis_size("exp")
    experts_here = w_in.shape[0]
    per_expert = owned // experts_here
    logits = jnp.dot(
        tokens.reshape(clips * tok_rows, width), router, preferred_element_type=jnp.float32
    ).reshape(clips, tok_rows, slot_total)
    slot_peak = lax.pmax(jnp.max(logits, axis=1), ("seq", "exp"))
    exp_terms = jnp.exp(logits - slot_peak[:, None, :])
    slot_mass = lax.psum(jnp.sum(exp_terms, axis=1), ("seq", "exp"))
    dispatch = exp_terms / slot_mass[:, None, :]
    dispatch_b = dispatch.astype(jnp.bfloat16)
    mixing = jax.nn.softmax(logits, axis=2)
    mixing_b = mixing.astype(jnp.bfloat16)
    inputs = jnp.einsum("cts,ctd->scd", dispatch_b, tokens, preferred_element_type=jnp.float32)
    grads = jnp.einsum("cts,ctd->scd", mixing_b, grad_out, preferred_element_type=jnp.float32)
    summed = lax.psum(jnp.concatenate([inputs, grads], axis=1), ("seq", "exp"))
    owner_sums = lax.dynamic_slice_in_dim(summed, lax.axis_index("exp") * owned, owned, 0)
    expert_rows = (
        owner_sums[:, :clips].astype(jnp.bfloat16).reshape(experts_here, per_expert * clips, width)
    )
    grad_rows = (
        owner_sums[:, clips:].astype(jnp.bfloat16).reshape(experts_here, per_expert * clips, width)
    )
    pre = jnp.einsum("erd,edh->erh", expert_rows, w_in, preferred_element_type=jnp.float32)
    hidden = jax.nn.gelu(pre).astype(jnp.bfloat16)
    expert_part = jnp.einsum("erh,ehd->erd", hidden, w_out, preferred_element_type=jnp.float32)
    hidden_grad = jnp.einsum("erd,ehd->erh", grad_rows, w_out, preferred_element_type=jnp.float32)
    pre_grad = jax.vjp(jax.nn.gelu, pre)[1](hidden_grad)[0].astype(jnp.bfloat16)
    grad_w_out = jnp.einsum(
        "erh,erd->ehd", hidden, grad_rows, preferred_element_type=jnp.float32
    ).astype(jnp.bfloat16)
    grad_w_in = jnp.einsum(
        "erd,erh->edh", expert_rows, pre_grad, preferred_element_type=jnp.float32
    ).astype(jnp.bfloat16)
    input_part = jnp.einsum("erh,edh->erd", pre_grad, w_in, preferred_element_type=jnp.float32)
    out_sums, in_sums = (
        lax.psum(expert_part.astype(jnp.bfloat16), "seq").astype(jnp.float32),
        lax.psum(input_part.astype(jnp.bfloat16), "seq").astype(jnp.float32),
    )
    slot_outputs = out_sums.astype(jnp.bfloat16).reshape(owned, clips, width)
    slot_in_grads = in_sums.astype(jnp.bfloat16).reshape(owned, clips, width)
    shard_rows = lax.all_gather(slot_outputs, "exp", axis=0, tiled=True)
    weights = mixing_b
    outputs = jnp.einsum("cts,scd->ctd", weights, shard_rows, preferred_element_type=jnp.float32)
    block = jnp.einsum("ctd,scd->cts", grad_out, shard_rows, preferred_element_type=jnp.float32)
    mixed = outputs
    mixing_grad = block
    shard_rows = lax.all_gather(slot_in_grads, "exp", axis=0, tiled=True)
    weights = dispatch_b
    outputs = jnp.einsum("cts,scd->ctd", weights, shard_rows, preferred_element_type=jnp.float32)
    block = jnp.einsum("ctd,scd->cts", tokens, shard_rows, preferred_element_type=jnp.float32)
    inner = lax.psum(jnp.sum(dispatch * block, axis=1), ("seq", "exp"))
    logit_grad = dispatch * (block - inner[:, None, :]) + mixing * (
        mixing_grad - jnp.sum(mixing * mixing_grad, axis=2, keepdims=True)
    )
    logit_b = logit_grad.astype(jnp.bfloat16)
    router_part = jnp.dot(
        logit_b.reshape(clips * tok_rows, slot_total), router.T, preferred_element_type=jnp.float32
    ).reshape(clips, tok_rows, width)
    grad_tokens = (outputs + router_part).astype(jnp.bfloat16)
    grad_router = lax.psum_scatter(
        jnp.einsum("ctd,cts->ds", tokens, logit_b, preferred_element_type=jnp.float32),
        ("seq", "exp"),
        scatter_dimension=0,
        tiled=True,
    )
    return (mixed.astype(jnp.bfloat16), grad_tokens, grad_router, grad_w_in, grad_w_out)


def solution(mesh):
    return jax.shard_map(
        on_device,
        mesh=mesh,
        in_specs=(
            P(None, ("seq", "exp"), None),
            P(),
            P("exp", None, "seq"),
            P("exp", "seq", None),
            P(None, ("seq", "exp"), None),
        ),
        out_specs=(
            P(None, ("seq", "exp"), None),
            P(None, ("seq", "exp"), None),
            P(("seq", "exp"), None),
            P("exp", None, "seq"),
            P("exp", "seq", None),
        ),
        check_vma=False,
    )
```

profile of v0, /device:TPU:0, one launch (start us, length us, event | category | flops | bytes accessed | tf_op | source)
XLA Modules:
  0.0 442.6 jit_solution(9276342582157628203)
XLA Ops:
  7.2 0.0 copy-start
  7.2 0.0 all-reduce.4.cloned.1.call-start
  7.2 1.8 copy-done
  9.1 2.1 fusion.37
  11.1 0.8 fusion.36
  12.0 41.9 %pmax.7 = f32[2,64]{1,0:T(2,128)S(1)} all-reduce(f32[2,64]{1,0:T(2,128)S(1)} %get-tuple-element.26), channel_id=1, replica_groups=mesh['seq'=4,'exp'=8] {'seq','exp'}, use_global_device_ids=true, to_apply=%region_3.0 | all-reduce | flops 128 | bytes 1024 | tf_op jit(solution)/shard_map/pmax | solution.py:16
  53.9 0.8 fusion.13
  54.7 40.3 %psum.35 = f32[2,64]{1,0:T(2,128)S(1)} all-reduce(f32[2,64]{1,0:T(2,128)} %fusion.13), channel_id=1, replica_groups=mesh['seq'=4,'exp'=8] {'seq','exp'}, use_global_device_ids=true, to_apply=%region_5.0 | all-reduce | flops 128 | bytes 1024 | tf_op jit(solution)/shard_map/psum | solution.py:18
  95.0 1.5 convolution_bitcast_fusion.1
  96.5 3.4 convolution_bitcast_fusion
  99.9 2.4 pad_maximum_fusion
  102.3 49.9 %all-reduce.5 = bf16[64,4,1024]{2,0,1:T(8,128)(2,1)} all-reduce(f32[64,4,1024]{2,0,1:T(8,128)} %pad_maximum_fusion), channel_id=1, replica_groups=mesh['seq'=4,'exp'=8] {'seq','exp'}, use_global_device_ids=true, to_apply=%region_6.0 | all-reduce | flops 262144 | bytes 1572864 | tf_op jit(solution)/shard_map/psum | solution.py:25
  152.2 0.8 dynamic-slice_convert_fusion
  153.0 0.6 fusion.35
  153.6 0.6 copy.20
  154.3 1.4 reshape.38
  155.7 1.4 copy.18
  157.1 1.4 reshape.36
  158.4 3.5 fusion.38
  162.0 0.0 copy-done.6
  162.0 3.5 fusion.28
  165.5 0.6 copy-done.4
  166.1 0.0 copy-done.1
  166.1 1.3 convolution_convert_fusion.4
  167.4 1.4 reshape.37
  168.8 1.4 copy.19
  170.1 4.0 convolution_convert_fusion.3
  174.2 1.4 reshape.39
  175.5 1.4 copy.21
  176.9 0.0 all-reduce.4.cloned.1.call-update
  176.9 0.0 reduce-scatter.4.cloned.1.call-start
  177.0 0.0 copy-start.5
  177.0 4.2 convolution_convert_fusion
  181.2 3.3 convolution_convert_fusion.1
  184.5 33.1 %all-reduce.4.cloned.1.call-done = (bf16[8,2,1024]{2,0,1:T(8,128)(2,1)}, bf16[8,2,1024]{2,0,1:T(8,128)(2,1)}) async-done(((bf16[8,2,1024]{2,0,1:T(8,128)(2,1)}, bf16[8,2,1024]{2,0,1:T(8,128)(2,1)}), (bf16[8,2,1024]{2,0,1:T(8,128)(2,1)}, bf16[8,2,1024]{2,0,1:T(8,128)(2,1)})) %all-reduce.4.cloned.1.call-update) | async-done | bytes 65552 | tf_op jit(solution)/shard_map/psum | solution.py:46
  217.6 14.6 %all_gather.7 = bf16[64,2,1024]{2,0,1:T(8,128)(2,1)S(1)} all-gather(bf16[8,2,1024]{2,0,1:T(8,128)(2,1)} %get-tuple-element.21), channel_id=1, replica_groups=mesh['seq'=4,'exp'=8] {'exp'}, dimensions={0}, use_global_device_ids=true | all-gather | bytes 294912 | tf_op jit(solution)/shard_map/all_gather | solution.py:57
  232.2 3.8 fusion.17
  236.0 2.4 multiply_reduce_fusion.1
  238.4 14.2 %all_gather.6 = bf16[64,2,1024]{2,0,1:T(8,128)(2,1)S(1)} all-gather(bf16[8,2,1024]{2,0,1:T(8,128)(2,1)S(1)} %copy-done.8), channel_id=1, replica_groups=mesh['seq'=4,'exp'=8] {'exp'}, dimensions={0}, use_global_device_ids=true | all-gather | bytes 294912 | tf_op jit(solution)/shard_map/all_gather | solution.py:51
  252.6 1.8 convolution_bitcast_fusion.2
  254.4 0.0 copy-done.3
  254.4 39.4 %psum.39 = f32[2,64]{1,0:T(2,128)} all-reduce(f32[2,64]{1,0:T(2,128)} %get-tuple-element.30), channel_id=1, replica_groups=mesh['seq'=4,'exp'=8] {'seq','exp'}, use_global_device_ids=true, to_apply=%region_10.0 | all-reduce | flops 128 | bytes 1024 | tf_op jit(solution)/shard_map/psum | solution.py:61
  293.8 3.0 convolution_bitcast_fusion.4
  296.8 2.0 copy.23
  298.8 0.0 reduce-scatter.4.cloned.1.call-update
  298.8 3.7 convolution_convert_fusion.2
  302.5 6.2 %add_convert_fusion = bf16[2,768,1024]{2,1,0:T(8,128)(2,1)} fusion(f32[2,768,1024]{2,1,0:T(8,128)} %fusion.17, f32[2,768,64]{1,2,0:T(8,128)} %convolution_bitcast_fusion.2, f32[2,768,64]{1,2,0:T(8,128)} %get-tuple-element.31, f32[2,64]{1,0:T(2,128)} %psum.39, bf16[1024,64]{0,1:T(8,128)(2,1)} %param.6, f32[2,768,64]{1,2,0:T(8,128)} %get-tuple-element.25, ...), kind=kOutput, calls=%fused_computation.2 | convolution fusion | flops 205555264 | bytes 11148800 | tf_op jit(solution)/shard_map/dot_general | solution.py:66
  308.7 127.1 %reduce-scatter.4.cloned.1.call-done = f32[32,64]{1,0:T(8,128)} async-done(((f32[1024,64]{1,0:T(8,128)}), f32[32,64]{1,0:T(8,128)}) %reduce-scatter.4.cloned.1.call-update) | async-done | bytes 8208
  (11 shorter events, 0.0 us)
Async XLA Ops:
  7.2 1.9 copy-start
  7.2 210.4 %all-reduce.4.cloned.1.call-start = ((), (), s32[]{:S(2)}) async-start(), calls=%async_computation.2 | async-start | bytes 131072 | tf_op jit(solution)/shard_map/psum | solution.py:46
  158.4 3.5 copy-start.6
  158.4 7.7 %copy-start.1 = (bf16[2,1024,1024]{2,1,0:T(8,128)(2,1)S(1)}, bf16[2,1024,1024]{2,1,0:T(8,128)(2,1)}, u32[]{:S(2)}) copy-start(bf16[2,1024,1024]{2,1,0:T(8,128)(2,1)} %param.8) | copy-start | bytes 12582916
  165.5 0.6 copy-start.4
  176.9 258.9 %reduce-scatter.4.cloned.1.call-start = ((), (), s32[]{:S(2)}) async-start(), calls=%async_computation.1 | async-start | bytes 540672
  177.0 4.2 copy-start.5
  177.0 4.2 copy-start.7
  232.2 6.2 %copy-start.8 = (bf16[8,2,1024]{2,0,1:T(8,128)(2,1)S(1)}, bf16[8,2,1024]{2,0,1:T(8,128)(2,1)}, u32[]{:S(2)}) copy-start(bf16[8,2,1024]{2,0,1:T(8,128)(2,1)} %get-tuple-element.20) | copy-start | bytes 98308
  232.2 20.4 %copy-start.2 = (bf16[2,768,1024]{2,1,0:T(8,128)(2,1)S(1)}, bf16[2,768,1024]{2,1,0:T(8,128)(2,1)}, u32[]{:S(2)}) copy-start(bf16[2,768,1024]{2,1,0:T(8,128)(2,1)} %param.9) | copy-start | bytes 9437188
  252.6 1.8 copy-start.3
Sparse Core Ops, SparseCore 0:
  177.0 40.5 all-reduce.3
  298.9 136.8 reduce-scatter.3
where the time goes:
time: 444 us; the launch traced here: 443 us
  blocking collectives  200 us (45%)
  waiting for transfers between devices  160 us (36%)
  matrix products  47.6 us (11%)
  local copies, waits for them, and re-layouts  16.2 us (4%)
  between operations  14.1 us (3%)
    unnamed x3, waiting for transfers between devices  127 us
    psum x1, blocking collectives, on_device(): summed = lax.psum(jnp.concatenate([inputs, grads], axis=1), ('seq', 'exp'))  49.9 us
    pmax x1, blocking collectives, on_device(): slot_peak = lax.pmax(jnp.max(logits, axis=1), ('seq', 'exp'))  41.9 us
    psum x1, blocking collectives, on_device(): slot_mass = lax.psum(jnp.sum(exp_terms, axis=1), ('seq', 'exp'))  40.3 us
    psum x1, blocking collectives, on_device(): inner = lax.psum(jnp.sum(dispatch * block, axis=1), ('seq', 'exp'))  39.4 us
    psum x1, waiting for transfers between devices, on_device(): lax.psum(expert_part.astype(jnp.bfloat16), 'seq').astype(jnp.float32)  33.1 us
    all_gather x1, blocking collectives, on_device(): shard_rows = lax.all_gather(slot_in_grads, 'exp', axis=0, tiled=True)  14.6 us
    all_gather x1, blocking collectives, on_device(): shard_rows = lax.all_gather(slot_outputs, 'exp', axis=0, tiled=True)  14.2 us
  transfers between devices with their start and end apart: 2, of which 2 were waited for; matrix products, arithmetic and copies ran while one was open for 4% of the time, Pallas kernels for 0%

commit v1 on v0

--- a/solution.py
+++ b/solution.py
@@ -2,6 +2,8 @@
 import jax.numpy as jnp
 from jax import lax
 from jax.sharding import PartitionSpec as P
+
+extend_spots = lambda tile_in: lax.psum(lax.psum(tile_in, "exp"), "seq")
 
 
 def on_device(tokens, router, w_in, w_out, grad_out):
@@ -58,7 +60,7 @@
     weights = dispatch_b
     outputs = jnp.einsum("cts,scd->ctd", weights, shard_rows, preferred_element_type=jnp.float32)
     block = jnp.einsum("ctd,scd->cts", tokens, shard_rows, preferred_element_type=jnp.float32)
-    inner = lax.psum(jnp.sum(dispatch * block, axis=1), ("seq", "exp"))
+    inner = extend_spots(jnp.sum(dispatch * block, axis=1))
     logit_grad = dispatch * (block - inner[:, None, :]) + mixing * (
         mixing_grad - jnp.sum(mixing * mixing_grad, axis=2, keepdims=True)
     )

time: 444 us -> 428 us (0.964)
  blocking collectives: 200 us -> 188 us
    psum x1 -> x2, blocking collectives: 39.4 us -> 27.1 us  [extend_spots = lambda tile_in: lax.psum(lax.psum(tile_in, 'exp'), 'seq')]
where the time goes in v1:
time: 428 us; the launch traced here: 426 us
  blocking collectives  188 us (44%)
  waiting for transfers between devices  156 us (36%)
  matrix products  47.6 us (11%)
  local copies, waits for them, and re-layouts  16.2 us (4%)
  between operations  14.1 us (3%)
    unnamed x3, waiting for transfers between devices  123 us
    psum x1, blocking collectives, on_device(): summed = lax.psum(jnp.concatenate([inputs, grads], axis=1), ('seq', 'exp'))  49.9 us
    pmax x1, blocking collectives, on_device(): slot_peak = lax.pmax(jnp.max(logits, axis=1), ('seq', 'exp'))  41.9 us
    psum x1, blocking collectives, on_device(): slot_mass = lax.psum(jnp.sum(exp_terms, axis=1), ('seq', 'exp'))  40.3 us
    psum x1, waiting for transfers between devices, on_device(): lax.psum(expert_part.astype(jnp.bfloat16), 'seq').astype(jnp.float32)  33.1 us
    psum x2, blocking collectives, extend_spots = lambda tile_in: lax.psum(lax.psum(tile_in, 'exp'), 'seq')  27.1 us
    all_gather x1, blocking collectives, on_device(): shard_rows = lax.all_gather(slot_in_grads, 'exp', axis=0, tiled=True)  14.6 us
    all_gather x1, blocking collectives, on_device(): shard_rows = lax.all_gather(slot_outputs, 'exp', axis=0, tiled=True)  14.2 us
  transfers between devices with their start and end apart: 2, of which 2 were waited for; matrix products, arithmetic and copies ran while one was open for 4% of the time, Pallas kernels for 0%

profile of v1, /device:TPU:0, one launch (start us, length us, event | category | flops | bytes accessed | tf_op | source)
XLA Modules:
  0.0 426.5 jit_solution(11053511454242505366)
XLA Ops:
  7.2 0.0 copy-start
  7.2 0.0 all-reduce.4.cloned.1.call-start
  7.2 1.8 copy-done
  9.1 2.1 fusion.37
  11.1 0.8 fusion.36
  12.0 41.9 %pmax.7 = f32[2,64]{1,0:T(2,128)S(1)} all-reduce(f32[2,64]{1,0:T(2,128)S(1)} %get-tuple-element.26), channel_id=1, replica_groups=mesh['seq'=4,'exp'=8] {'seq','exp'}, use_global_device_ids=true, to_apply=%region_3.0 | all-reduce | flops 128 | bytes 1024 | tf_op jit(solution)/shard_map/pmax | solution.py:18
  53.9 0.8 fusion.13
  54.7 40.3 %psum.42 = f32[2,64]{1,0:T(2,128)S(1)} all-reduce(f32[2,64]{1,0:T(2,128)} %fusion.13), channel_id=1, replica_groups=mesh['seq'=4,'exp'=8] {'seq','exp'}, use_global_device_ids=true, to_apply=%region_5.0 | all-reduce | flops 128 | bytes 1024 | tf_op jit(solution)/shard_map/psum | solution.py:20
  95.0 1.5 convolution_bitcast_fusion.1
  96.5 3.4 convolution_bitcast_fusion
  99.9 2.4 pad_maximum_fusion
  102.3 49.9 %all-reduce.5 = bf16[64,4,1024]{2,0,1:T(8,128)(2,1)} all-reduce(f32[64,4,1024]{2,0,1:T(8,128)} %pad_maximum_fusion), channel_id=1, replica_groups=mesh['seq'=4,'exp'=8] {'seq','exp'}, use_global_device_ids=true, to_apply=%region_6.0 | all-reduce | flops 262144 | bytes 1572864 | tf_op jit(solution)/shard_map/psum | solution.py:27
  152.2 0.8 dynamic-slice_convert_fusion
  153.0 0.6 fusion.35
  153.6 0.6 copy.20
  154.3 1.4 reshape.38
  155.7 1.4 copy.18
  157.1 1.4 reshape.36
  158.4 3.5 fusion.38
  162.0 0.0 copy-done.6
  162.0 3.5 fusion.28
  165.5 0.6 copy-done.4
  166.1 1.3 convolution_convert_fusion.4
  167.4 1.4 reshape.37
  168.8 1.4 copy.19
  170.1 4.0 convolution_convert_fusion.3
  174.2 1.4 reshape.39
  175.5 1.4 copy.21
  176.9 0.0 all-reduce.4.cloned.1.call-update
  176.9 0.0 reduce-scatter.4.cloned.1.call-start
  177.0 0.0 copy-start.5
  177.0 4.2 convolution_convert_fusion
  181.2 3.3 convolution_convert_fusion.1
  184.5 33.1 %all-reduce.4.cloned.1.call-done = (bf16[8,2,1024]{2,0,1:T(8,128)(2,1)}, bf16[8,2,1024]{2,0,1:T(8,128)(2,1)}) async-done(((bf16[8,2,1024]{2,0,1:T(8,128)(2,1)}, bf16[8,2,1024]{2,0,1:T(8,128)(2,1)}), (bf16[8,2,1024]{2,0,1:T(8,128)(2,1)}, bf16[8,2,1024]{2,0,1:T(8,128)(2,1)})) %all-reduce.4.cloned.1.call-update) | async-done | bytes 65552 | tf_op jit(solution)/shard_map/psum | solution.py:48
  217.6 14.6 %all_gather.7 = bf16[64,2,1024]{2,0,1:T(8,128)(2,1)S(1)} all-gather(bf16[8,2,1024]{2,0,1:T(8,128)(2,1)} %get-tuple-element.21), channel_id=1, replica_groups=mesh['seq'=4,'exp'=8] {'exp'}, dimensions={0}, use_global_device_ids=true | all-gather | bytes 294912 | tf_op jit(solution)/shard_map/all_gather | solution.py:59
  232.2 3.8 fusion.17
  236.0 2.4 multiply_reduce_fusion.1
  238.4 14.2 %all_gather.6 = bf16[64,2,1024]{2,0,1:T(8,128)(2,1)S(1)} all-gather(bf16[8,2,1024]{2,0,1:T(8,128)(2,1)S(1)} %copy-done.8), channel_id=1, replica_groups=mesh['seq'=4,'exp'=8] {'exp'}, dimensions={0}, use_global_device_ids=true | all-gather | bytes 294912 | tf_op jit(solution)/shard_map/all_gather | solution.py:53
  252.6 1.8 convolution_bitcast_fusion.2
  254.4 0.0 copy-done.3
  254.4 17.5 %psum.46 = f32[2,64]{1,0:T(2,128)} all-reduce(f32[2,64]{1,0:T(2,128)} %get-tuple-element.30), channel_id=1, replica_groups=mesh['seq'=4,'exp'=8] {'exp'}, use_global_device_ids=true, to_apply=%region_10.0 | all-reduce | flops 128 | bytes 1024 | tf_op jit(solution)/shard_map/psum | solution.py:6
  271.9 9.6 %psum.47 = f32[2,64]{1,0:T(2,128)} all-reduce(f32[2,64]{1,0:T(2,128)} %psum.46), channel_id=1, replica_groups=mesh['seq'=4,'exp'=8] {'seq'}, use_global_device_ids=true, to_apply=%region_11.0 | all-reduce | flops 128 | bytes 1024 | tf_op jit(solution)/shard_map/psum | solution.py:6
  281.5 3.0 convolution_bitcast_fusion.4
  284.6 2.0 copy.23
  286.5 0.0 reduce-scatter.4.cloned.1.call-update
  286.6 3.7 convolution_convert_fusion.2
  290.2 6.2 %add_convert_fusion = bf16[2,768,1024]{2,1,0:T(8,128)(2,1)} fusion(f32[2,768,1024]{2,1,0:T(8,128)} %fusion.17, f32[2,768,64]{1,2,0:T(8,128)} %convolution_bitcast_fusion.2, f32[2,768,64]{1,2,0:T(8,128)} %get-tuple-element.31, f32[2,64]{1,0:T(2,128)} %psum.47, bf16[1024,64]{0,1:T(8,128)(2,1)} %param.6, f32[2,768,64]{1,2,0:T(8,128)} %get-tuple-element.25, ...), kind=kOutput, calls=%fused_computation.2 | convolution fusion | flops 205555264 | bytes 11148800 | tf_op jit(solution)/shard_map/dot_general | solution.py:68
  296.5 123.2 %reduce-scatter.4.cloned.1.call-done = f32[32,64]{1,0:T(8,128)} async-done(((f32[1024,64]{1,0:T(8,128)}), f32[32,64]{1,0:T(8,128)}) %reduce-scatter.4.cloned.1.call-update) | async-done | bytes 8208
  (12 shorter events, 0.0 us)
Async XLA Ops:
  7.2 1.9 copy-start
  7.2 210.4 %all-reduce.4.cloned.1.call-start = ((), (), s32[]{:S(2)}) async-start(), calls=%async_computation.2 | async-start | bytes 131072 | tf_op jit(solution)/shard_map/psum | solution.py:48
  158.4 3.5 copy-start.6
  158.4 7.7 %copy-start.1 = (bf16[2,1024,1024]{2,1,0:T(8,128)(2,1)S(1)}, bf16[2,1024,1024]{2,1,0:T(8,128)(2,1)}, u32[]{:S(2)}) copy-start(bf16[2,1024,1024]{2,1,0:T(8,128)(2,1)} %param.8) | copy-start | bytes 12582916
  165.5 0.6 copy-start.4
  176.9 242.7 %reduce-scatter.4.cloned.1.call-start = ((), (), s32[]{:S(2)}) async-start(), calls=%async_computation.1 | async-start | bytes 540672
  177.0 4.2 copy-start.5
  177.0 4.2 copy-start.7
  232.2 6.2 %copy-start.8 = (bf16[8,2,1024]{2,0,1:T(8,128)(2,1)S(1)}, bf16[8,2,1024]{2,0,1:T(8,128)(2,1)}, u32[]{:S(2)}) copy-start(bf16[8,2,1024]{2,0,1:T(8,128)(2,1)} %get-tuple-element.20) | copy-start | bytes 98308
  232.2 20.4 %copy-start.2 = (bf16[2,768,1024]{2,1,0:T(8,128)(2,1)S(1)}, bf16[2,768,1024]{2,1,0:T(8,128)(2,1)}, u32[]{:S(2)}) copy-start(bf16[2,768,1024]{2,1,0:T(8,128)(2,1)} %param.9) | copy-start | bytes 9437188
  252.6 1.8 copy-start.3
Sparse Core Ops, SparseCore 0:
  177.0 40.5 all-reduce.3
  286.7 132.8 reduce-scatter.3
